TPU v7x, 512 devices: a 8x2x16 block of a 8x8x16 slice. The times are simulated.
512 devices in a mesh: groups: 2 (over y), ctx: 32 (over z, core), tp: 8 (over x).
Axes of the slice: x: 8, y: 2, z: 16, core: 2. Of those that a mesh axis runs over, the one named last changes fastest.
The devices are a block of a 8x8x16 slice.
Arguments:
- q_nope: bfloat16 [4096, 16384], P(('groups', 'ctx'), 'tp'), parts along dimension 0, may hold values from -6 to 6
- q_rope: bfloat16 [4096, 8192], P(('groups', 'ctx'), 'tp'), parts along dimension 0, may hold values from -6 to 6
- c_kv: bfloat16 [4096, 512], P(('groups', 'ctx')), parts along dimension 0, may hold values from -6 to 46.4
- k_rope: bfloat16 [4096, 64], P(('groups', 'ctx')), parts along dimension 0, may hold values from -6 to 6
- positions: int32 [4096], P(('groups', 'ctx')), parts along dimension 0, may hold values from 0 to 2047, as said below
- w_uk: bfloat16 [128, 128, 512], P('tp', 'ctx'), may hold values from -0.5 to 0.5
- w_uv: bfloat16 [128, 512, 128], P('tp', 'ctx'), may hold values from -0.25 to 0.25
- w_out: bfloat16 [16384, 7168], P('tp', 'ctx'), may hold values from -0.125 to 0.125
Outputs:
- attn_proj: bfloat16 [4096, 7168], P(('groups', 'tp'), 'ctx'), parts along dimension 0
There are 2 independent parts, one for each index of `groups`. A program takes and returns all parts, laid end to end along the dimension named above; an argument that names none is the same for every part. Nothing has to cross between parts.
Inputs may be any that keep to these rules, and one draw needn't show every extreme that they name: The positions are the 2048 integers 0 to 2047, each once; every aligned block of 32 rows holds consecutive ascending positions.
All inputs are finite; a program needn't handle non-finite values.
Results may differ from a plain program's by a relative error of at most 0.015.
Values may be sent and summed in bfloat16 or wider, within the bound.
No kernel may reach another device: no remote copies, remote signals or barrier semaphores. Data moves between devices by JAX's collectives and lax.ppermute only.
A program may use at most 64 MiB of HBM per device.

v0:
```python
import jax
import jax.numpy as jnp
from jax import lax
from jax.sharding import PartitionSpec as P


def laid_out(blocks, dim):
    blocks = jnp.moveaxis(blocks, 0, dim)
    lengths = blocks.shape
    return blocks.reshape(*lengths[:dim], lengths[dim] * lengths[dim + 1], *lengths[dim + 2 :])


def gather_together(arrays, axis, dims):
    flat = jnp.concatenate([a.reshape(-1) for a in arrays])
    lines, at, gathered = (lax.all_gather(flat, axis), 0, [])
    for a, dim in zip(arrays, dims):
        blocks = lines[:, at : at + a.size].reshape(-1, *a.shape)
        gathered.append(laid_out(blocks, dim))
        at += a.size
    return tuple(gathered)


def in_blocks(x, dim, size):
    before, after = (x.shape[:dim], x.shape[dim + 1 :])
    return jnp.moveaxis(x.reshape(*before, size, -1, *after), dim, 0)


def sent_and_summed(x, axis, dim):
    blocks = in_blocks(x, dim, lax.axis_size(axis))
    arrived = lax.all_to_all(blocks, axis, split_axis=0, concat_axis=0, tiled=True)
    return arrived.astype(jnp.float32).sum(axis=0)


def rotate(values, position):
    half_dim = values.shape[-1] // 2
    freqs = 10000.0 ** (-jnp.arange(half_dim, dtype=jnp.float32) / half_dim)
    angles = position.astype(jnp.float32)[..., None] * freqs
    cosine = jnp.cos(angles)
    sine = jnp.sin(angles)
    first_half = values[..., :half_dim].astype(jnp.float32)
    second_half = values[..., half_dim:].astype(jnp.float32)
    return jnp.concatenate(
        [first_half * cosine - second_half * sine, second_half * cosine + first_half * sine],
        axis=-1,
    )


def on_device(q_nope, q_rope, c_kv, k_rope, positions, w_uk, w_uv, w_out):
    tok_count = q_nope.shape[0]
    head_count = w_uk.shape[0]
    latent = c_kv.shape[1]
    up_key, up_value = gather_together((w_uk, w_uv), "ctx", (1, 1))
    nope_dim = up_key.shape[1]
    rope_dim = k_rope.shape[1]
    softmax_scale = (nope_dim + rope_dim) ** (-0.5)
    q_parts = q_nope.reshape(tok_count, head_count, nope_dim)
    q_lat = jnp.einsum("thn,hnl->thl", q_parts, up_key, preferred_element_type=jnp.float32).astype(
        jnp.bfloat16
    )
    q_rot = rotate(q_rope.reshape(tok_count, head_count, rope_dim), positions[:, None]).astype(
        jnp.bfloat16
    )
    k_rot = rotate(k_rope, positions).astype(jnp.bfloat16)
    key_rows = jnp.concatenate([c_kv, k_rot], axis=1)
    queries = jnp.concatenate([q_lat, q_rot], axis=2).reshape(
        tok_count * head_count, latent + rope_dim
    )
    query_pos = jnp.repeat(positions, head_count)
    row_total = tok_count * head_count
    key_part = lax.all_gather(key_rows, "ctx", axis=0, tiled=True)
    key_pos = lax.all_gather(positions, "ctx", axis=0, tiled=True)
    run_max = jnp.full((row_total,), -1e30, jnp.float32)
    scores = (
        jnp.einsum("rk,sk->rs", queries, key_part, preferred_element_type=jnp.float32)
        * softmax_scale
    )
    visible = key_pos[None, :] <= query_pos[:, None]
    new_max = jnp.maximum(run_max, jnp.max(jnp.where(visible, scores, -1e30), axis=1))
    weights = jnp.where(visible, jnp.exp(scores - new_max[:, None]), 0.0)
    new_sum = jnp.sum(weights, axis=1)
    added = jnp.dot(
        weights.astype(jnp.bfloat16), key_part[:, :latent], preferred_element_type=jnp.float32
    )
    o_lat = (added / new_sum[:, None]).astype(jnp.bfloat16).reshape(tok_count, head_count, latent)
    head_out = jnp.einsum("thl,hlv->thv", o_lat, up_value, preferred_element_type=jnp.float32)
    rows_out = head_out.astype(jnp.bfloat16).reshape(tok_count, -1)
    partial_value = jnp.dot(
        lax.all_gather(rows_out, "ctx", axis=0, tiled=True),
        w_out,
        preferred_element_type=jnp.float32,
    )
    summed = sent_and_summed(partial_value.astype(jnp.bfloat16), "tp", 0)
    return summed.astype(jnp.bfloat16)


def solution(mesh):
    in_specs = (
        P(("groups", "ctx"), "tp"),
        P(("groups", "ctx"), "tp"),
        P(("groups", "ctx"), None),
        P(("groups", "ctx"), None),
        P(("groups", "ctx")),
        P("tp", "ctx", None),
        P("tp", "ctx", None),
        P("tp", "ctx"),
    )
    out_specs = P(("groups", "tp"), "ctx")
    return jax.shard_map(
        on_device, mesh=mesh, in_specs=in_specs, out_specs=out_specs, check_vma=False
    )
```

profile of v0, /device:TPU:65, one launch (start us, length us, event | category | flops | bytes accessed | tf_op | source)
XLA Modules:
  0.0 328.4 jit_solution(10513221402875094891)
XLA Ops:
  6.6 0.9 copy.33
  7.5 1.5 pad_maximum_fusion.1
  9.1 0.7 convert_element_type.45
  9.8 1.0 fusion.20
  10.8 1.6 pad_maximum_fusion.2
  12.5 1.3 dynamic-slice
  14.5 0.9 dynamic-update-slice
  15.4 57.5 %all-reduce = s32[2048]{0:T(1024)S(1)} all-reduce(s32[2048]{0:T(1024)S(1)} %dynamic-update-slice), channel_id=1, replica_groups=mesh['groups'=2,'ctx'=32,'tp'=8] {'ctx'}, use_global_device_ids=true, to_apply=%add | all-reduce | flops 2048 | bytes 16384
  72.9 0.7 broadcast_in_dim.11
  73.7 1.1 reshape.118
  75.0 0.2 fusion.14
  75.2 45.3 %all-gather.9.cloned.1.call-done = bf16[2097152]{0:T(1024)(128)(2,1)} async-done(((bf16[65536]{0:T(1024)(128)(2,1)}), bf16[2097152]{0:T(1024)(128)(2,1)}) %all-gather.9.cloned.1.call-update) | async-done | bytes 4194320 | tf_op jit(solution)/shard_map/all_gather | solution.py:15
  120.4 5.6 %reshape.123 = bf16[32,65536]{1,0:T(8,128)(2,1)} reshape(bf16[2097152]{0:T(1024)(128)(2,1)} %all-gather.9.cloned.1.call-done) | data formatting | bytes 8388608 | tf_op jit(solution)/shard_map/all_gather | solution.py:15
  126.0 4.4 %fusion.25 = (bf16[32,32768]{1,0:T(8,128)(2,1)}, bf16[4,8,256,128]{3,1,2,0:T(8,128)(2,1)}) fusion(bf16[32,65536]{1,0:T(8,128)(2,1)} %reshape.123), kind=kLoop, calls=%fused_computation.44 | loop fusion | bytes 8388608 | tf_op jit(solution)/shard_map/slice | solution.py:17
  130.4 3.3 %reshape.115 = bf16[32,16,4,512]{3,2,1,0:T(4,128)(2,1)S(1)} reshape(bf16[32,32768]{1,0:T(8,128)(2,1)} %get-tuple-element.5) | data formatting | bytes 4194304 | tf_op jit(solution)/shard_map/reshape | solution.py:17
  133.8 2.3 copy.20
  136.1 2.5 reshape.116
  138.6 1.4 fusion.6
  140.0 0.2 pad_maximum_fusion
  140.3 1.8 copy.24
  142.1 0.5 copy.34
  142.6 0.5 copy.19
  143.1 49.6 %all-gather.5.cloned.1.call-done = bf16[2048,576]{1,0:T(8,128)(2,1)} async-done(((bf16[64,576]{1,0:T(8,128)(2,1)}), bf16[2048,576]{1,0:T(8,128)(2,1)}) %all-gather.5.cloned.1.call-update) | async-done | bytes 2359312 | tf_op jit(solution)/shard_map/all_gather | solution.py:70
  192.8 5.9 %fusion = (f32[1024]{0:T(1024)S(1)}, f32[1024,2048]{1,0:T(8,128)S(1)}) fusion(s32[2048]{0:T(1024)S(1)} %all-reduce, s32[1024]{0:T(1024)S(1)} %le.16, bf16[1024,576]{1,0:T(8,128)(2,1)} %bitcast.43, bf16[2048,576]{1,0:T(8,128)(2,1)} %all-gather.5.cloned.1.call-done), kind=kOutput, calls=%fused_computation.2 | convolution fusion | flops 2424306688 | bytes 11943936 | tf_op jit(solution)/shard_map/rk,sk->rs/dot_general | solution.py:74
  198.7 2.8 fusion.1
  201.5 2.5 divide_convert_fusion
  204.0 1.4 fusion.7
  205.4 0.8 copy.48
  206.3 77.1 %all-gather.7.cloned.1.call-done = bf16[2048,2048]{1,0:T(8,128)(2,1)} async-done(((bf16[64,2048]{1,0:T(8,128)(2,1)}), bf16[2048,2048]{1,0:T(8,128)(2,1)}) %all-gather.7.cloned.1.call-update) | async-done | bytes 8388624 | tf_op jit(solution)/shard_map/all_gather | solution.py:88
  283.4 6.0 %convolution_convert_fusion = bf16[2048,224]{0,1:T(8,128)(2,1)S(1)} fusion(bf16[2048,2048]{1,0:T(8,128)(2,1)} %all-gather.7.cloned.1.call-done, bf16[2048,224]{0,1:T(8,128)(2,1)S(1)} %copy-done), kind=kOutput, calls=%fused_computation.6 | convolution fusion | flops 1879506944 | bytes 10223616 | tf_op jit(solution)/shard_map/dot_general | solution.py:87
  289.5 31.6 %all_to_all.5 = bf16[8,256,224]{1,2,0:T(8,128)(2,1)S(1)} all-to-all(bf16[8,256,224]{1,2,0:T(8,128)(2,1)S(1)} %bitcast.42), channel_id=1, replica_groups=mesh['groups'=2,'ctx'=32,'tp'=8] {'tp'}, dimensions={0} | all-to-all | bytes 1835008 | tf_op jit(solution)/shard_map/all_to_all | solution.py:30
  321.1 0.8 reduce_sum.22
  (18 shorter events, 0.6 us)
Async XLA Ops:
  6.5 276.9 %copy-start = (bf16[2048,224]{0,1:T(8,128)(2,1)S(1)}, bf16[2048,224]{0,1:T(8,128)(2,1)}, u32[]{:S(2)}) copy-start(bf16[2048,224]{0,1:T(8,128)(2,1)} %param.15) | copy-start | bytes 2752516
  6.6 113.9 %all-gather.9.cloned.1.call-start = ((), (), s32[]{:S(2)}) async-start(), calls=%async_computation.3 | async-start | bytes 4325376 | tf_op jit(solution)/shard_map/all_gather | solution.py:15
  9.0 183.7 %all-gather.5.cloned.1.call-start = ((), (), s32[]{:S(2)}) async-start(), calls=%async_computation.1 | async-start | bytes 2703360 | tf_op jit(solution)/shard_map/all_gather | solution.py:70
  12.4 271.0 %all-gather.7.cloned.1.call-start = ((), (), s32[]{:S(2)}) async-start(), calls=%async_computation.2 | async-start | bytes 8650752 | tf_op jit(solution)/shard_map/all_gather | solution.py:88
  140.0 2.1 copy-start.1
  198.7 2.8 copy-start.2
Sparse Core Ops, SparseCore 0:
  9.5 110.9 all-gather.8
  122.6 70.1 all-gather.4
  206.4 76.9 all-gather.6
where the time goes:
time: 329 us; the launch traced here: 328 us
  waiting for transfers between devices  172 us (52%)
  blocking collectives  89.1 us (27%)
  local copies, waits for them, and re-layouts  27.1 us (8%)
  matrix products  17.2 us (5%)
  between operations  14 us (4%)
  other arithmetic  8.72 us (3%)
    all_gather x1, waiting for transfers between devices, on_device(): lax.all_gather(rows_out, 'ctx', axis=0, tiled=True)  77.1 us
    unnamed x1, blocking collectives  57.5 us
    all_gather x1, waiting for transfers between devices, on_device(): key_part = lax.all_gather(key_rows, 'ctx', axis=0, tiled=True)  49.6 us
    all_gather x1, waiting for transfers between devices, gather_together(): lines, at, gathered = (lax.all_gather(flat, axis), 0, [])  45.3 us
    all_to_all x1, blocking collectives, sent_and_summed(): lax.all_to_all(blocks, axis, split_axis=0, concat_axis=0, tiled=True)  31.6 us
  transfers between devices with their start and end apart: 3, of which 3 were waited for; matrix products, arithmetic and copies ran while one was open for 9% of the time, Pallas kernels for 0%

commit v1 on v0

--- a/solution.py
+++ b/solution.py
@@ -67,7 +67,9 @@
     )
     query_pos = jnp.repeat(positions, head_count)
     row_total = tok_count * head_count
-    key_part = lax.all_gather(key_rows, "ctx", axis=0, tiled=True)
+    key_part = jnp.concatenate(
+        lax.all_to_all(jnp.stack([key_rows] * lax.axis_size("ctx")), "ctx", 0, 0), axis=0
+    )
     key_pos = lax.all_gather(positions, "ctx", axis=0, tiled=True)
     run_max = jnp.full((row_total,), -1e30, jnp.float32)
     scores = (

time: 329 us -> 376 us (1.14)
  waiting for transfers between devices: 172 us -> 84.1 us
  blocking collectives: 89.1 us -> 176 us
  starting transfers between devices: 0.13 us -> 46.2 us
    unnamed x1, blocking collectives: 57.5 us -> 145 us
    all_gather x1 -> x0, waiting for transfers between devices: 49.6 us -> none  [on_device(): key_part = lax.all_gather(key_rows, 'ctx', axis=0, tiled=True)]
    all_to_all x0 -> x1, starting transfers between devices: none -> 46.2 us  [on_device(): lax.all_to_all(jnp.stack([key_rows] * lax.axis_size('ctx')), 'ctx', 0, 0)]
    all_gather x1, waiting for transfers between devices: 45.3 us -> 0.02 us  [gather_together(): lines, at, gathered = (lax.all_gather(flat, axis), 0, [])]
    all_gather x1, waiting for transfers between devices: 77.1 us -> 84 us  [on_device(): lax.all_gather(rows_out, 'ctx', axis=0, tiled=True)]
  transfers between devices with their start and end apart: 3 -> 3, of which waited for: 3 -> 1; matrix products, arithmetic and copies ran while one was open for 9% -> 8% of each run, Pallas kernels for 0% -> 0%
where the time goes in v1:
time: 376 us; the launch traced here: 375 us
  blocking collectives  176 us (47%)
  waiting for transfers between devices  84.1 us (22%)
  starting transfers between devices  46.2 us (12%)
  local copies, waits for them, and re-layouts  26.7 us (7%)
  matrix products  18.9 us (5%)
  between operations  14.3 us (4%)
  other arithmetic  8.09 us (2%)
    unnamed x1, blocking collectives  145 us
    all_gather x1, waiting for transfers between devices, on_device(): lax.all_gather(rows_out, 'ctx', axis=0, tiled=True)  84 us
    all_to_all x1, starting transfers between devices, on_device(): lax.all_to_all(jnp.stack([key_rows] * lax.axis_size('ctx')), 'ctx', 0, 0)  46.2 us
    all_to_all x1, blocking collectives, sent_and_summed(): lax.all_to_all(blocks, axis, split_axis=0, concat_axis=0, tiled=True)  31.6 us
  transfers between devices with their start and end apart: 3, of which 1 were waited for; matrix products, arithmetic and copies ran while one was open for 8% of the time, Pallas kernels for 0%

profile of v1, /device:TPU:65, one launch (start us, length us, event | category | flops | bytes accessed | tf_op | source)
XLA Modules:
  0.0 374.8 jit_solution(17312169179815345282)
XLA Ops:
  6.6 0.9 copy.33
  7.5 1.5 pad_maximum_fusion.1
  9.0 0.7 convert_element_type.45
  9.7 1.0 fusion.20
  10.7 0.9 pad_maximum_fusion.2
  11.6 1.9 stack.2
  13.6 46.2 %all-to-all-start = ((bf16[32,64,576]{2,1,0:T(8,128)(2,1)}), bf16[32,64,576]{2,1,0:T(8,128)(2,1)}, u32[]{:S(2)}, u32[]{:S(2)}) async-start(bf16[32,64,576]{2,1,0:T(8,128)(2,1)} %stack.2), calls=%async_computation | async-start | bytes 5242880 | tf_op jit(solution)/shard_map/all_to_all | solution.py:71
  60.0 0.2 reshape.123
  60.2 1.3 dynamic-slice
  62.1 0.3 dynamic-update-slice
  62.4 144.9 %all-reduce = s32[2048]{0:T(1024)S(1)} all-reduce(s32[2048]{0:T(1024)S(1)} %dynamic-update-slice), channel_id=1, replica_groups=mesh['groups'=2,'ctx'=32,'tp'=8] {'ctx'}, use_global_device_ids=true, to_apply=%add | all-reduce | flops 2048 | bytes 16384
  207.3 0.1 fusion.26
  207.4 0.2 fusion.14
  207.7 5.6 %reshape.129 = bf16[32,65536]{1,0:T(8,128)(2,1)} reshape(bf16[2097152]{0:T(1024)(128)(2,1)} %all-gather.6.cloned.1.call-done) | data formatting | bytes 8388608 | tf_op jit(solution)/shard_map/all_gather | solution.py:15
  213.2 4.4 %fusion.25 = (bf16[32,32768]{1,0:T(8,128)(2,1)}, bf16[4,8,256,128]{3,1,2,0:T(8,128)(2,1)}) fusion(bf16[32,65536]{1,0:T(8,128)(2,1)} %reshape.129), kind=kLoop, calls=%fused_computation.44 | loop fusion | bytes 8388608 | tf_op jit(solution)/shard_map/slice | solution.py:17
  217.7 3.3 reshape.120
  221.0 2.3 copy.20
  223.3 2.5 reshape.121
  225.9 1.4 fusion.6
  227.3 0.2 pad_maximum_fusion
  227.5 1.8 copy.24
  229.3 0.5 copy.34
  229.8 0.5 copy.19
  230.4 5.9 %fusion = (f32[1024]{0:T(1024)S(1)}, f32[1024,2048]{1,0:T(8,128)S(1)}) fusion(s32[2048]{0:T(1024)S(1)} %all-reduce, s32[1024]{0:T(1024)S(1)} %le.16, bf16[1024,576]{1,0:T(8,128)(2,1)} %bitcast.44, bf16[2048,576]{1,0:T(8,128)(2,1)} %bitcast.7), kind=kOutput, calls=%fused_computation.2 | convolution fusion | flops 2424306688 | bytes 11943936 | tf_op jit(solution)/shard_map/rk,sk->rs/dot_general | solution.py:76
  236.3 2.8 fusion.1
  239.1 4.1 %divide_convert_fusion = bf16[1024,512]{1,0:T(8,128)(2,1)S(1)} fusion(f32[1024]{0:T(1024)S(1)} %fusion.1, bf16[2048,576]{1,0:T(8,128)(2,1)} %bitcast.7, f32[1024,2048]{1,0:T(8,128)S(1)} %get-tuple-element.16, f32[1024]{0:T(1024)S(1)} %broadcast_maximum_fusion, s32[2048]{0:T(1024)S(1)} %all-reduce, s32[1024]{0:T(1024)S(1)} %le.16), kind=kOutput, calls=%fused_computation.9 | convolution fusion | flops 2159017984 | bytes 11554816 | tf_op jit(solution)/shard_map/dot_general | solution.py:83
  243.2 1.4 fusion.7
  244.6 0.8 copy.48
  245.5 84.0 %all-gather.4.cloned.1.call-done = bf16[2048,2048]{1,0:T(8,128)(2,1)} async-done(((bf16[64,2048]{1,0:T(8,128)(2,1)}), bf16[2048,2048]{1,0:T(8,128)(2,1)}) %all-gather.4.cloned.1.call-update) | async-done | bytes 8388624 | tf_op jit(solution)/shard_map/all_gather | solution.py:90
  329.5 6.0 %convolution_convert_fusion = bf16[2048,224]{0,1:T(8,128)(2,1)S(1)} fusion(bf16[2048,2048]{1,0:T(8,128)(2,1)} %all-gather.4.cloned.1.call-done, bf16[2048,224]{0,1:T(8,128)(2,1)S(1)} %copy-done), kind=kOutput, calls=%fused_computation.6 | convolution fusion | flops 1879506944 | bytes 10223616 | tf_op jit(solution)/shard_map/dot_general | solution.py:89
  335.6 31.6 %all_to_all.10 = bf16[8,256,224]{1,2,0:T(8,128)(2,1)S(1)} all-to-all(bf16[8,256,224]{1,2,0:T(8,128)(2,1)S(1)} %bitcast.43), channel_id=1, replica_groups=mesh['groups'=2,'ctx'=32,'tp'=8] {'tp'}, dimensions={0} | all-to-all | bytes 1835008 | tf_op jit(solution)/shard_map/all_to_all | solution.py:30
  367.2 0.8 reduce_sum.22
  (20 shorter events, 0.4 us)
Async XLA Ops:
  6.5 322.9 %copy-start = (bf16[2048,224]{0,1:T(8,128)(2,1)S(1)}, bf16[2048,224]{0,1:T(8,128)(2,1)}, u32[]{:S(2)}) copy-start(bf16[2048,224]{0,1:T(8,128)(2,1)} %param.15) | copy-start | bytes 2752516
  6.6 201.1 %all-gather.6.cloned.1.call-start = ((), (), s32[]{:S(2)}) async-start(), calls=%async_computation.3 | async-start | bytes 4325376 | tf_op jit(solution)/shard_map/all_gather | solution.py:15
  13.6 46.2 %copy-start.3 = (s32[64]{0:T(128)S(1)}, s32[64]{0:T(128)}, u32[]{:S(2)}) copy-start(s32[64]{0:T(128)} %param.12) | copy-start | bytes 772
  13.6 46.4 %copy-start.2 = (bf16[64,1024]{1,0:T(8,128)(2,1)S(1)}, bf16[64,1024]{1,0:T(8,128)(2,1)}, u32[]{:S(2)}) copy-start(bf16[64,1024]{1,0:T(8,128)(2,1)} %param.9) | copy-start | bytes 393220
  13.6 216.8 %all-to-all-start = ((bf16[32,64,576]{2,1,0:T(8,128)(2,1)}), bf16[32,64,576]{2,1,0:T(8,128)(2,1)}, u32[]{:S(2)}, u32[]{:S(2)}) async-start(bf16[32,64,576]{2,1,0:T(8,128)(2,1)} %stack.2), calls=%async_computation | async-start | bytes 5242880 | tf_op jit(solution)/shard_map/all_to_all | solution.py:71
  59.7 269.7 %all-gather.4.cloned.1.call-start = ((), (), s32[]{:S(2)}) async-start(), calls=%async_computation.2 | async-start | bytes 8650752 | tf_op jit(solution)/shard_map/all_gather | solution.py:90
  227.2 2.1 copy-start.1
Sparse Core Ops, SparseCore 0:
  9.5 177.9 all-gather.5
  245.6 83.8 all-gather.3

commit v2 on v0

--- a/solution.py
+++ b/solution.py
@@ -2,6 +2,14 @@
 import jax.numpy as jnp
 from jax import lax
 from jax.sharding import PartitionSpec as P
+
+
+def tiled_gather(shard, axis, dim):
+    length = lax.axis_size(axis)
+    repeats = [length if d == dim else 1 for d in range(shard.ndim)]
+    return lax.all_to_all(
+        jnp.tile(shard, repeats), axis, split_axis=dim, concat_axis=dim, tiled=True
+    )
 
 
 def laid_out(blocks, dim):
@@ -85,9 +93,7 @@
     head_out = jnp.einsum("thl,hlv->thv", o_lat, up_value, preferred_element_type=jnp.float32)
     rows_out = head_out.astype(jnp.bfloat16).reshape(tok_count, -1)
     partial_value = jnp.dot(
-        lax.all_gather(rows_out, "ctx", axis=0, tiled=True),
-        w_out,
-        preferred_element_type=jnp.float32,
+        tiled_gather(rows_out, "ctx", 0), w_out, preferred_element_type=jnp.float32
     )
     summed = sent_and_summed(partial_value.astype(jnp.bfloat16), "tp", 0)
     return summed.astype(jnp.bfloat16)

time: 329 us -> 627 us (1.91)
  blocking collectives: 89.1 us -> 467 us
  waiting for transfers between devices: 172 us -> 95.2 us
    all_to_all x0 -> x1, blocking collectives: none -> 378 us  [tiled_gather(): lax.all_to_all(jnp.tile(shard, repeats), axis, split_axis=dim, concat_axi...]
    all_gather x1 -> x0, waiting for transfers between devices: 77.1 us -> none  [on_device(): lax.all_gather(rows_out, 'ctx', axis=0, tiled=True)]
  transfers between devices with their start and end apart: 3 -> 2, of which waited for: 3 -> 2; matrix products, arithmetic and copies ran while one was open for 9% -> 5% of each run, Pallas kernels for 0% -> 0%
where the time goes in v2:
time: 627 us; the launch traced here: 626 us
  blocking collectives  467 us (74%)
  waiting for transfers between devices  95.2 us (15%)
  local copies, waits for them, and re-layouts  27.4 us (4%)
  between operations  14.3 us (2%)
  matrix products  13.8 us (2%)
  other arithmetic  8.73 us (1%)
    all_to_all x1, blocking collectives, tiled_gather(): lax.all_to_all(jnp.tile(shard, repeats), axis, split_axis=dim, concat_axi...  378 us
    unnamed x1, blocking collectives  57.4 us
    all_gather x1, waiting for transfers between devices, on_device(): key_part = lax.all_gather(key_rows, 'ctx', axis=0, tiled=True)  49.7 us
    all_gather x1, waiting for transfers between devices, gather_together(): lines, at, gathered = (lax.all_gather(flat, axis), 0, [])  45.4 us
    all_to_all x1, blocking collectives, sent_and_summed(): lax.all_to_all(blocks, axis, split_axis=0, concat_axis=0, tiled=True)  31 us
  transfers between devices with their start and end apart: 2, of which 2 were waited for; matrix products, arithmetic and copies ran while one was open for 5% of the time, Pallas kernels for 0%

profile of v2, /device:TPU:65, one launch (start us, length us, event | category | flops | bytes accessed | tf_op | source)
XLA Modules:
  0.0 626.0 jit_solution(11325682776673063179)
XLA Ops:
  6.6 0.9 copy.33
  7.5 1.5 pad_maximum_fusion.1
  9.1 0.7 convert_element_type.45
  9.8 1.0 fusion.20
  10.8 1.6 pad_maximum_fusion.2
  12.4 1.3 dynamic-slice
  14.4 0.9 dynamic-update-slice
  15.3 57.4 %all-reduce = s32[2048]{0:T(1024)S(1)} all-reduce(s32[2048]{0:T(1024)S(1)} %dynamic-update-slice), channel_id=1, replica_groups=mesh['groups'=2,'ctx'=32,'tp'=8] {'ctx'}, use_global_device_ids=true, to_apply=%add | all-reduce | flops 2048 | bytes 16384
  72.7 0.7 broadcast_in_dim.11
  73.5 1.1 reshape.122
  74.8 0.2 fusion.14
  75.0 45.4 %all-gather.6.cloned.1.call-done = bf16[2097152]{0:T(1024)(128)(2,1)} async-done(((bf16[65536]{0:T(1024)(128)(2,1)}), bf16[2097152]{0:T(1024)(128)(2,1)}) %all-gather.6.cloned.1.call-update) | async-done | bytes 4194320 | tf_op jit(solution)/shard_map/all_gather | solution.py:23
  120.4 5.5 reshape.126
  126.0 4.4 fusion.25
  130.4 3.3 reshape.119
  133.7 2.3 copy.20
  136.0 2.5 reshape.120
  138.6 1.4 fusion.6
  140.0 0.2 pad_maximum_fusion
  140.2 1.8 copy.24
  142.0 0.5 copy.34
  142.5 0.5 copy.19
  143.1 49.7 %all-gather.4.cloned.1.call-done = bf16[2048,576]{1,0:T(8,128)(2,1)} async-done(((bf16[64,576]{1,0:T(8,128)(2,1)}), bf16[2048,576]{1,0:T(8,128)(2,1)}) %all-gather.4.cloned.1.call-update) | async-done | bytes 2359312 | tf_op jit(solution)/shard_map/all_gather | solution.py:78
  192.8 5.9 fusion
  198.7 2.8 fusion.1
  201.5 2.5 divide_convert_fusion
  204.0 1.4 fusion.7
  205.5 1.1 tile.9
  206.5 378.2 %all_to_all.14 = bf16[32,64,2048]{2,1,0:T(8,128)(2,1)S(1)} all-to-all(bf16[32,64,2048]{2,1,0:T(8,128)(2,1)S(1)} %tile.9), channel_id=1, replica_groups=mesh['groups'=2,'ctx'=32,'tp'=8] {'ctx'}, dimensions={0} | all-to-all | bytes 16777216 | tf_op jit(solution)/shard_map/all_to_all | solution.py:10
  584.7 2.6 convolution_convert_fusion
  587.4 31.0 %all_to_all.15 = bf16[8,256,224]{1,2,0:T(8,128)(2,1)S(1)} all-to-all(bf16[8,256,224]{1,2,0:T(8,128)(2,1)S(1)} %bitcast.44), channel_id=1, replica_groups=mesh['groups'=2,'ctx'=32,'tp'=8] {'tp'}, dimensions={0} | all-to-all | bytes 1835008 | tf_op jit(solution)/shard_map/all_to_all | solution.py:38
  618.4 0.8 reduce_sum.22
  (17 shorter events, 0.5 us)
Async XLA Ops:
  6.5 578.2 %copy-start = (bf16[2048,224]{0,1:T(8,128)(2,1)S(1)}, bf16[2048,224]{0,1:T(8,128)(2,1)}, u32[]{:S(2)}) copy-start(bf16[2048,224]{0,1:T(8,128)(2,1)} %param.15) | copy-start | bytes 2752516
  6.6 113.9 %all-gather.6.cloned.1.call-start = ((), (), s32[]{:S(2)}) async-start(), calls=%async_computation.3 | async-start | bytes 4325376 | tf_op jit(solution)/shard_map/all_gather | solution.py:23
  9.1 183.7 %all-gather.4.cloned.1.call-start = ((), (), s32[]{:S(2)}) async-start(), calls=%async_computation.2 | async-start | bytes 2703360 | tf_op jit(solution)/shard_map/all_gather | solution.py:78
  140.0 2.1 copy-start.1
  198.7 2.8 copy-start.2
Sparse Core Ops, SparseCore 0:
  9.5 110.8 all-gather.5
  122.6 70.1 all-gather.3
